TPU v7x, 128 devices: a whole 4x4x4 slice. The times are simulated.
128 devices in a mesh: scen: 32 (over z_hi, x, y), col: 4 (over z_lo, core).
Axes of the slice: x: 4, y: 4, z: 4 (z_hi: 2, z_lo: 2; z = z_hi * 2 + z_lo), core: 2. Of those that a mesh axis runs over, the one named last changes fastest.
Arguments:
- tech: bfloat16 [128, 2048, 4096], P('scen', None, 'col'), may hold values from -0.0234375 to 0.0234375
- recourse: bfloat16 [128, 2048, 1024], P('scen', None, 'col'), may hold values from -0.125 to 0.125
- rhs: float32 [32, 128, 2048], P(None, 'scen'), may hold values from -6 to 6
- cost_first: float32 [4096], P('col'), may hold values from -6 to 6
- cost_second: float32 [128, 1024], P('scen', 'col'), may hold values from -6 to 6
- cone_id: int32 [128, 2048], P('scen'), may hold values from 0 to 127, never falling along the last dimension, each value on 1 to 64 neighbouring positions
Outputs:
- first_section: float32 [32, 4096], P(None, 'col')
- second_section: float32 [32, 128, 1024], P(None, 'scen', 'col')
- slack: float32 [32, 128, 2048], P(None, 'scen', 'col')
- dual: float32 [32, 128, 2048], P(None, 'scen', 'col')
Inputs may be any that keep to these rules, and one draw needn't show every extreme that they name: Along the rows of a scenario cone_id never falls; a cone holds 1 to 64 rows.
All inputs are finite; a program needn't handle non-finite values.
Results may differ from a plain program's by a relative error of at most 0.014.
Values may be sent and summed in bfloat16 or wider, within the bound.
A program may use at most 128 MiB of HBM per device.

v0:
```python
import functools

import jax
import jax.numpy as jnp
from jax import lax
from jax.sharding import Mesh
from jax.sharding import PartitionSpec as P

NCONE = 128
ITERS = 3
CG_STEPS = 3
SCEN = ("scen_0", "scen_1", "scen_2")
COL = ("col_0", "col_1")
SCEN_COL = ("scen_0", "scen_1", "scen_2", "col_0", "col_1")


def copy_for_each(value, axis):
    count = lax.axis_size(axis)
    return lax.all_to_all(
        jnp.broadcast_to(value[None], (count, *value.shape)), axis, 0, 0, tiled=True
    )


def laid_out(blocks, dim):
    blocks = jnp.moveaxis(blocks, 0, dim)
    shape = blocks.shape
    return blocks.reshape(*shape[:dim], shape[dim] * shape[dim + 1], *shape[dim + 2 :])


def gather_directly(value, axis, dim):
    blocks = copy_for_each(value, axis)
    return laid_out(blocks, dim)


def split_up(value, dim, count):
    shape = value.shape
    blocks = value.reshape(*shape[:dim], count, shape[dim] // count, *shape[dim + 1 :])
    return jnp.moveaxis(blocks, dim, 0)


def sum_at_owner(value, axis, dim):
    blocks = split_up(value, dim, lax.axis_size(axis))
    arrived = lax.all_to_all(blocks, axis, split_axis=0, concat_axis=0, tiled=True)
    return arrived.sum(axis=0)


def with_halo(value, sides, width):
    for axis, dim in sides:
        count, length = (lax.axis_size(axis), value.shape[dim])
        up = [(i, (i + 1) % count) for i in range(count - 1)]
        down = [(j, i) for i, j in up]
        last = lax.slice_in_dim(value, length - width, length, axis=dim)
        leading = lax.slice_in_dim(value, 0, width, axis=dim)
        before = lax.ppermute(last, axis, up)
        after = lax.ppermute(leading, axis, down)
        value = jnp.concatenate([before, value, after], axis=dim)
    return value


def by_axis(value, axes):
    return functools.reduce(lax.psum, axes, value)


def cone_factors(lead, tail):
    norm_tail = jnp.sqrt(tail)
    inside = norm_tail <= lead
    polar = norm_tail <= -lead
    safe = jnp.where(norm_tail > 0.0, norm_tail, 1.0)
    middle = 0.5 * (lead + norm_tail)
    head = jnp.where(inside, lead, jnp.where(polar, 0.0, middle))
    scale = jnp.where(inside, 1.0, jnp.where(polar, 0.0, middle / safe))
    return (head, scale)


def body(tech, recourse, rhs, cost_first, cost_second, cone_id):
    f32 = jnp.float32
    bf16 = jnp.bfloat16
    n_scen = lax.axis_size(SCEN)
    n_col = lax.axis_size(COL)
    batch = rhs.shape[0]
    scen_local = tech.shape[0]
    rows = tech.shape[1]
    first_cols = tech.shape[2]
    tech_flat = tech.reshape(scen_local * rows, first_cols)
    starts = jnp.concatenate(
        [jnp.ones((scen_local, 1), f32), (cone_id[:, 1:] != cone_id[:, :-1]).astype(f32)], axis=1
    )
    labels = lax.broadcasted_iota(jnp.int32, (1, 1, NCONE), 2)
    onehot = (cone_id[:, :, None] == labels).astype(f32)
    part_rows = rows // n_col
    row_start = lax.axis_index(COL) * part_rows
    starts_here = lax.dynamic_slice_in_dim(starts, row_start, part_rows, 1)
    onehot_here = lax.dynamic_slice_in_dim(onehot, row_start, part_rows, 1)
    rhs_here = lax.dynamic_slice_in_dim(rhs, row_start, part_rows, 2)
    row_weight = 1.0
    share_cols = first_cols // n_scen
    cost_here = lax.dynamic_slice_in_dim(
        cost_first, lax.axis_index(SCEN) * share_cols, share_cols, 0
    )
    first_weight = 1.0
    start_rows = starts_here[None]

    def full_rows(values_bf):
        return gather_directly(values_bf, COL, 2)

    def couple(partial_value):
        return sum_at_owner(partial_value, SCEN, 1)

    def adjoint(rows_bf):
        first_part = jnp.dot(
            rows_bf.reshape(batch, scen_local * rows), tech_flat, preferred_element_type=f32
        )
        second_part = jnp.einsum("bsm,smk->bsk", rows_bf, recourse, preferred_element_type=f32)
        return (first_part, second_part)

    def local_squares(first_vec, second_vec):
        return first_weight * jnp.sum(first_vec * first_vec, axis=1) + jnp.sum(
            second_vec * second_vec, axis=(1, 2)
        )

    def total_norm(first_vec, second_vec):
        return by_axis(local_squares(first_vec, second_vec), SCEN_COL)

    here_rows = rhs_here.shape[2]
    first_sol = jnp.zeros((batch, share_cols), f32)
    second_sol = jnp.zeros((batch, scen_local, recourse.shape[2]), f32)
    slack = jnp.zeros((batch, scen_local, here_rows), f32)
    dual = jnp.zeros((batch, scen_local, here_rows), f32)
    image = jnp.zeros((batch, scen_local, here_rows), f32)
    for outer in range(ITERS):
        resid_rows = (rhs_here - slack - dual - image).astype(bf16)
        back_first, back_second = adjoint(full_rows(resid_rows))
        res_first = couple(back_first) - cost_here[None, :]
        res_second = back_second - cost_second[None]
        res_norm = total_norm(res_first, res_second)
        dir_first, dir_second = (res_first, res_second)
        for step in range(CG_STEPS):
            dir_first_bf = gather_directly(dir_first.astype(bf16), SCEN, 1)
            forward_partial_value = lax.dot_general(
                dir_first_bf, tech_flat, (((1,), (1,)), ((), ())), preferred_element_type=f32
            )
            forward_partial_value = forward_partial_value.reshape(batch, scen_local, rows)
            image_step = sum_at_owner(
                forward_partial_value
                + jnp.einsum(
                    "bsk,smk->bsm", dir_second.astype(bf16), recourse, preferred_element_type=f32
                ),
                COL,
                2,
            )
            curv_term = local_squares(dir_first, dir_second) + row_weight * jnp.sum(
                image_step * image_step, axis=(1, 2)
            )
            curv = by_axis(curv_term, SCEN_COL)
            alpha = res_norm / curv
            first_sol = first_sol + alpha[:, None] * dir_first
            second_sol = second_sol + alpha[:, None, None] * dir_second
            image = image + alpha[:, None, None] * image_step
            if step + 1 < CG_STEPS:
                back_first, back_second = adjoint(full_rows(image_step.astype(bf16)))
                res_first = res_first - alpha[:, None] * (dir_first + couple(back_first))
                res_second = res_second - alpha[:, None, None] * (dir_second + back_second)
                new_norm = total_norm(res_first, res_second)
                ratio = new_norm / res_norm
                dir_first = res_first + ratio[:, None] * dir_first
                dir_second = res_second + ratio[:, None, None] * dir_second
                res_norm = new_norm
        values = rhs_here - image - dual
        project_lead = jnp.einsum("bsm,smc->bsc", values * start_rows, onehot_here)
        project_tail = jnp.einsum("bsm,smc->bsc", values * values * (1.0 - start_rows), onehot_here)
        stacked = jnp.stack([project_lead, project_tail], axis=0)[None]
        widened = with_halo(stacked, ((COL, 0),), 1)
        summed = jnp.sum(widened, axis=0)
        project_lead = summed[0]
        project_tail = summed[1]
        head, scale = cone_factors(project_lead, project_tail)
        head_rows = jnp.einsum("bsc,smc->bsm", head, onehot_here)
        scale_rows = jnp.einsum("bsc,smc->bsm", scale, onehot_here)
        slack = start_rows * head_rows + (1.0 - start_rows) * values * scale_rows
        dual = dual + image + slack - rhs_here
    first_out = lax.all_gather(first_sol, SCEN, axis=1, tiled=True)
    return (first_out, second_sol, slack, dual)


def solution(mesh):
    torus = Mesh(
        mesh.devices.reshape(2, 4, 4, 2, 2), ("scen_0", "scen_1", "scen_2", "col_0", "col_1")
    )
    placed = (
        P(SCEN, None, COL),
        P(SCEN, None, COL),
        P(None, SCEN, None),
        P(COL),
        P(SCEN, COL),
        P(SCEN, None),
    )
    return jax.shard_map(
        body,
        mesh=torus,
        in_specs=placed,
        out_specs=(P(None, COL), P(None, SCEN, COL), P(None, SCEN, COL), P(None, SCEN, COL)),
        check_vma=False,
    )
```

profile of v0, /device:TPU:0, one launch (start us, length us, event | category | flops | bytes accessed | tf_op | source)
XLA Modules:
  0.0 1471.9 jit_solution(6910024510363846244)
XLA Ops:
  6.5 20.9 %copy.96 = bf16[1024,8192]{1,0:T(8,128)(2,1)} copy(bf16[1024,8192]{0,1:T(8,128)(2,1)} %bitcast.430) | data formatting | bytes 33554432 | tf_op jit(solution)/shard_map/dot_general | solution.py:110
  28.2 16.8 %convolution_bitcast_fusion.17 = f32[32,32,32]{2,1,0:T(8,128)S(1)} fusion(bf16[32,8192,1]{1,0,2:T(8,128)(2,1)S(1)} %reshape.594, bf16[32,32,8192]{2,1,0:T(8,128)(2,1)} %bitcast.431), kind=kOutput, calls=%fused_computation.26 | convolution fusion | flops 536870912 | bytes 17432576 | tf_op jit(solution)/shard_map/dot_general | solution.py:110
  84.3 10.8 fusion.148
  98.7 16.9 %all_to_all.180 = f32[4,32,4,512]{3,1,2,0:T(8,128)S(1)} all-to-all(f32[4,32,4,512]{3,1,2,0:T(8,128)S(1)} %bitcast.465), channel_id=1, replica_groups=mesh['scen_0'=2,'scen_1'=4,'scen_2'=4,'col_0'=2,'col_1'=2] {'col_0','col..., dimensions={0} | all-to-all | bytes 2097152 | tf_op jit(solution)/shard_map/all_to_all | solution.py:43
  155.2 16.8 %convolution_bitcast_fusion.16 = f32[32,32,32]{2,1,0:T(8,128)S(1)} fusion(bf16[32,8192,1]{1,0,2:T(8,128)(2,1)S(1)} %reshape.596, bf16[32,32,8192]{2,1,0:T(8,128)(2,1)} %bitcast.432), kind=kOutput, calls=%fused_computation.25 | convolution fusion | flops 536870912 | bytes 17432576 | tf_op jit(solution)/shard_map/dot_general | solution.py:110
  237.6 10.8 fusion.149
  252.0 16.9 %all_to_all.181 = f32[4,32,4,512]{3,1,2,0:T(8,128)S(1)} all-to-all(f32[4,32,4,512]{3,1,2,0:T(8,128)S(1)} %bitcast.466), channel_id=1, replica_groups=mesh['scen_0'=2,'scen_1'=4,'scen_2'=4,'col_0'=2,'col_1'=2] {'col_0','col..., dimensions={0} | all-to-all | bytes 2097152 | tf_op jit(solution)/shard_map/all_to_all | solution.py:43
  309.4 16.8 %convolution_bitcast_fusion.15 = f32[32,32,32]{2,1,0:T(8,128)S(1)} fusion(bf16[32,8192,1]{1,0,2:T(8,128)(2,1)S(1)} %reshape.598, bf16[32,32,8192]{2,1,0:T(8,128)(2,1)} %bitcast.433), kind=kOutput, calls=%fused_computation.24 | convolution fusion | flops 536870912 | bytes 17432576 | tf_op jit(solution)/shard_map/dot_general | solution.py:110
  393.8 10.8 fusion.150
  413.2 13.9 all-to-all-done.11
  468.5 14.6 all_to_all.182
  483.9 16.8 %convolution_bitcast_fusion.14 = f32[32,32,32]{2,1,0:T(8,128)S(1)} fusion(bf16[32,8192,1]{1,0,2:T(8,128)(2,1)S(1)} %reshape.600, bf16[32,32,8192]{2,1,0:T(8,128)(2,1)} %bitcast.434), kind=kOutput, calls=%fused_computation.23 | convolution fusion | flops 536870912 | bytes 17432576 | tf_op jit(solution)/shard_map/dot_general | solution.py:110
  532.3 10.8 fusion.151
  546.7 16.9 %all_to_all.183 = f32[4,32,4,512]{3,1,2,0:T(8,128)S(1)} all-to-all(f32[4,32,4,512]{3,1,2,0:T(8,128)S(1)} %bitcast.467), channel_id=1, replica_groups=mesh['scen_0'=2,'scen_1'=4,'scen_2'=4,'col_0'=2,'col_1'=2] {'col_0','col..., dimensions={0} | all-to-all | bytes 2097152 | tf_op jit(solution)/shard_map/all_to_all | solution.py:43
  604.6 16.8 %convolution_bitcast_fusion.13 = f32[32,32,32]{2,1,0:T(8,128)S(1)} fusion(bf16[32,8192,1]{1,0,2:T(8,128)(2,1)S(1)} %reshape.602, bf16[32,32,8192]{2,1,0:T(8,128)(2,1)} %bitcast.435), kind=kOutput, calls=%fused_computation.22 | convolution fusion | flops 536870912 | bytes 17432576 | tf_op jit(solution)/shard_map/dot_general | solution.py:110
  688.5 10.8 fusion.152
  702.9 16.9 %all_to_all.184 = f32[4,32,4,512]{3,1,2,0:T(8,128)S(1)} all-to-all(f32[4,32,4,512]{3,1,2,0:T(8,128)S(1)} %bitcast.468), channel_id=1, replica_groups=mesh['scen_0'=2,'scen_1'=4,'scen_2'=4,'col_0'=2,'col_1'=2] {'col_0','col..., dimensions={0} | all-to-all | bytes 2097152 | tf_op jit(solution)/shard_map/all_to_all | solution.py:43
  762.5 16.8 %convolution_bitcast_fusion.12 = f32[32,32,32]{2,1,0:T(8,128)S(1)} fusion(bf16[32,8192,1]{1,0,2:T(8,128)(2,1)S(1)} %reshape.604, bf16[32,32,8192]{2,1,0:T(8,128)(2,1)} %bitcast.436), kind=kOutput, calls=%fused_computation.21 | convolution fusion | flops 536870912 | bytes 17432576 | tf_op jit(solution)/shard_map/dot_general | solution.py:110
  833.3 12.8 all_to_all.185
  866.6 13.5 all-to-all-done.23
  923.9 14.6 all_to_all.186
  939.3 16.8 %convolution_bitcast_fusion.11 = f32[32,32,32]{2,1,0:T(8,128)S(1)} fusion(bf16[32,8192,1]{1,0,2:T(8,128)(2,1)S(1)} %reshape.606, bf16[32,32,8192]{2,1,0:T(8,128)(2,1)} %bitcast.437), kind=kOutput, calls=%fused_computation.20 | convolution fusion | flops 536870912 | bytes 17432576 | tf_op jit(solution)/shard_map/dot_general | solution.py:110
  987.9 10.8 fusion.154
  1002.3 16.9 %all_to_all.187 = f32[4,32,4,512]{3,1,2,0:T(8,128)S(1)} all-to-all(f32[4,32,4,512]{3,1,2,0:T(8,128)S(1)} %bitcast.469), channel_id=1, replica_groups=mesh['scen_0'=2,'scen_1'=4,'scen_2'=4,'col_0'=2,'col_1'=2] {'col_0','col..., dimensions={0} | all-to-all | bytes 2097152 | tf_op jit(solution)/shard_map/all_to_all | solution.py:43
  1058.2 16.8 %convolution_bitcast_fusion.10 = f32[32,32,32]{2,1,0:T(8,128)S(1)} fusion(bf16[32,8192,1]{1,0,2:T(8,128)(2,1)S(1)} %reshape.608, bf16[32,32,8192]{2,1,0:T(8,128)(2,1)} %bitcast.438), kind=kOutput, calls=%fused_computation.19 | convolution fusion | flops 536870912 | bytes 17432576 | tf_op jit(solution)/shard_map/dot_general | solution.py:110
  1141.2 10.8 fusion.155
  1155.6 16.9 %all_to_all.188 = f32[4,32,4,512]{3,1,2,0:T(8,128)S(1)} all-to-all(f32[4,32,4,512]{3,1,2,0:T(8,128)S(1)} %bitcast.470), channel_id=1, replica_groups=mesh['scen_0'=2,'scen_1'=4,'scen_2'=4,'col_0'=2,'col_1'=2] {'col_0','col..., dimensions={0} | all-to-all | bytes 2097152 | tf_op jit(solution)/shard_map/all_to_all | solution.py:43
  1213.0 16.8 %convolution_bitcast_fusion.9 = f32[32,32,32]{2,1,0:T(8,128)S(1)} fusion(bf16[32,8192,1]{1,0,2:T(8,128)(2,1)S(1)} %reshape.610, bf16[32,32,8192]{2,1,0:T(8,128)(2,1)} %bitcast.439), kind=kOutput, calls=%fused_computation.18 | convolution fusion | flops 536870912 | bytes 17432576 | tf_op jit(solution)/shard_map/dot_general | solution.py:110
  1281.8 13.1 all_to_all.189
  1295.5 10.8 fusion.156
  1315.8 13.0 all-to-all-done.35
  1375.1 91.0 %all_gather.3 = f32[32,1024]{0,1:T(8,128)S(1)} all-gather(f32[32,32]{0,1:T(8,128)S(1)} %copy.140), channel_id=1, replica_groups=mesh['scen_0'=2,'scen_1'=4,'scen_2'=4,'col_0'=2,'col_1'=2] {'scen_0','sc..., dimensions={1}, use_global_device_ids=true | all-gather | bytes 135168 | tf_op jit(solution)/shard_map/all_gather | solution.py:181
  (512 shorter events, 922.7 us)
Async XLA Ops:
  3.0 24.4 %all-to-all-start = ((bf16[4,32,4,512]{3,2,1,0:T(4,128)(2,1)}), bf16[4,32,4,512]{3,2,1,0:T(4,128)(2,1)S(1)}, u32[]{:S(2)}, u32[]{:S(2)}) async-start(bf16[4,32,4,512]{3,2,1,0:T(4,128)(2,1)} %broadcast_in_dim.60), calls=%async_computation | async-start | bytes 1048576 | tf_op jit(solution)/shard_map/all_to_all | solution.py:19
  46.0 20.8 %all-to-all-start.1 = ((f32[32,1,1024]{2,1,0:T(1,128)}), f32[32,1,1024]{2,1,0:T(1,128)S(1)}, u32[]{:S(2)}, u32[]{:S(2)}) async-start(f32[32,1,1024]{2,1,0:T(1,128)} %reshape.630), calls=%async_computation.1 | async-start | bytes 262144 | tf_op jit(solution)/shard_map/all_to_all | solution.py:43
  69.6 14.2 all-to-all-start.2
  116.9 37.2 %all-to-all-start.4 = ((bf16[4,32,4,512]{3,2,1,0:T(4,128)(2,1)}), bf16[4,32,4,512]{3,2,1,0:T(4,128)(2,1)S(1)}, u32[]{:S(2)}, u32[]{:S(2)}) async-start(bf16[4,32,4,512]{3,2,1,0:T(4,128)(2,1)} %broadcast_in_dim.62), calls=%async_computation.4 | async-start | bytes 1048576 | tf_op jit(solution)/shard_map/all_to_all | solution.py:19
  173.4 15.0 %all-to-all-start.5 = ((f32[32,1,1024]{2,1,0:T(1,128)}), f32[32,1,1024]{2,1,0:T(1,128)S(1)}, u32[]{:S(2)}, u32[]{:S(2)}) async-start(f32[32,1,1024]{2,1,0:T(1,128)} %reshape.634), calls=%async_computation.5 | async-start | bytes 262144 | tf_op jit(solution)/shard_map/all_to_all | solution.py:43
  223.3 13.7 all-to-all-start.6
  270.2 38.0 %all-to-all-start.8 = ((bf16[4,32,4,512]{3,2,1,0:T(4,128)(2,1)}), bf16[4,32,4,512]{3,2,1,0:T(4,128)(2,1)S(1)}, u32[]{:S(2)}, u32[]{:S(2)}) async-start(bf16[4,32,4,512]{3,2,1,0:T(4,128)(2,1)} %broadcast_in_dim.64), calls=%async_computation.8 | async-start | bytes 1048576 | tf_op jit(solution)/shard_map/all_to_all | solution.py:19
  327.6 15.0 %all-to-all-start.9 = ((f32[32,1,1024]{2,1,0:T(1,128)}), f32[32,1,1024]{2,1,0:T(1,128)S(1)}, u32[]{:S(2)}, u32[]{:S(2)}) async-start(f32[32,1,1024]{2,1,0:T(1,128)} %reshape.638), calls=%async_computation.9 | async-start | bytes 262144 | tf_op jit(solution)/shard_map/all_to_all | solution.py:43
  379.1 14.1 all-to-all-start.10
  409.2 17.9 %all-to-all-start.11 = ((f32[4,32,4,512]{3,1,2,0:T(8,128)}), f32[4,32,4,512]{3,1,2,0:T(8,128)S(1)}, u32[]{:S(2)}, u32[]{:S(2)}) async-start(f32[4,32,4,512]{3,1,2,0:T(8,128)} %bitcast.425), calls=%async_computation.11 | async-start | bytes 2097152 | tf_op jit(solution)/shard_map/all_to_all | solution.py:43
  460.7 4.3 collective-permute-start.1
  462.0 4.0 collective-permute-start
  501.7 14.1 all-to-all-start.13
  518.0 13.7 all-to-all-start.14
  564.8 36.8 %all-to-all-start.16 = ((bf16[4,32,4,512]{3,2,1,0:T(4,128)(2,1)}), bf16[4,32,4,512]{3,2,1,0:T(4,128)(2,1)S(1)}, u32[]{:S(2)}, u32[]{:S(2)}) async-start(bf16[4,32,4,512]{3,2,1,0:T(4,128)(2,1)} %broadcast_in_dim.71), calls=%async_computation.16 | async-start | bytes 1048576 | tf_op jit(solution)/shard_map/all_to_all | solution.py:19
  622.8 15.6 %all-to-all-start.17 = ((f32[32,1,1024]{2,1,0:T(1,128)}), f32[32,1,1024]{2,1,0:T(1,128)S(1)}, u32[]{:S(2)}, u32[]{:S(2)}) async-start(f32[32,1,1024]{2,1,0:T(1,128)} %reshape.646), calls=%async_computation.17 | async-start | bytes 262144 | tf_op jit(solution)/shard_map/all_to_all | solution.py:43
  673.8 14.2 all-to-all-start.18
  721.2 38.4 %all-to-all-start.20 = ((bf16[4,32,4,512]{3,2,1,0:T(4,128)(2,1)}), bf16[4,32,4,512]{3,2,1,0:T(4,128)(2,1)S(1)}, u32[]{:S(2)}, u32[]{:S(2)}) async-start(bf16[4,32,4,512]{3,2,1,0:T(4,128)(2,1)} %broadcast_in_dim.73), calls=%async_computation.20 | async-start | bytes 1048576 | tf_op jit(solution)/shard_map/all_to_all | solution.py:19
  780.7 15.1 %all-to-all-start.21 = ((f32[32,1,1024]{2,1,0:T(1,128)}), f32[32,1,1024]{2,1,0:T(1,128)S(1)}, u32[]{:S(2)}, u32[]{:S(2)}) async-start(f32[32,1,1024]{2,1,0:T(1,128)} %reshape.650), calls=%async_computation.21 | async-start | bytes 262144 | tf_op jit(solution)/shard_map/all_to_all | solution.py:43
  862.2 17.9 %all-to-all-start.23 = ((f32[4,32,4,512]{3,1,2,0:T(8,128)}), f32[4,32,4,512]{3,1,2,0:T(8,128)S(1)}, u32[]{:S(2)}, u32[]{:S(2)}) async-start(f32[4,32,4,512]{3,1,2,0:T(8,128)} %bitcast.419), calls=%async_computation.23 | async-start | bytes 2097152 | tf_op jit(solution)/shard_map/all_to_all | solution.py:43
  914.8 4.3 collective-permute-start.3
  916.1 4.0 collective-permute-start.2
  957.0 13.9 all-to-all-start.25
  973.2 14.1 all-to-all-start.26
  1020.4 36.6 %all-to-all-start.28 = ((bf16[4,32,4,512]{3,2,1,0:T(4,128)(2,1)}), bf16[4,32,4,512]{3,2,1,0:T(4,128)(2,1)S(1)}, u32[]{:S(2)}, u32[]{:S(2)}) async-start(bf16[4,32,4,512]{3,2,1,0:T(4,128)(2,1)} %broadcast_in_dim.78), calls=%async_computation.28 | async-start | bytes 1048576 | tf_op jit(solution)/shard_map/all_to_all | solution.py:19
  1076.3 15.6 %all-to-all-start.29 = ((f32[32,1,1024]{2,1,0:T(1,128)}), f32[32,1,1024]{2,1,0:T(1,128)S(1)}, u32[]{:S(2)}, u32[]{:S(2)}) async-start(f32[32,1,1024]{2,1,0:T(1,128)} %reshape.658), calls=%async_computation.29 | async-start | bytes 262144 | tf_op jit(solution)/shard_map/all_to_all | solution.py:43
  1126.9 13.7 all-to-all-start.30
  1173.9 37.9 %all-to-all-start.32 = ((bf16[4,32,4,512]{3,2,1,0:T(4,128)(2,1)}), bf16[4,32,4,512]{3,2,1,0:T(4,128)(2,1)S(1)}, u32[]{:S(2)}, u32[]{:S(2)}) async-start(bf16[4,32,4,512]{3,2,1,0:T(4,128)(2,1)} %broadcast_in_dim.80), calls=%async_computation.32 | async-start | bytes 1048576 | tf_op jit(solution)/shard_map/all_to_all | solution.py:19
  1231.1 15.0 %all-to-all-start.33 = ((f32[32,1,1024]{2,1,0:T(1,128)}), f32[32,1,1024]{2,1,0:T(1,128)S(1)}, u32[]{:S(2)}, u32[]{:S(2)}) async-start(f32[32,1,1024]{2,1,0:T(1,128)} %reshape.662), calls=%async_computation.33 | async-start | bytes 262144 | tf_op jit(solution)/shard_map/all_to_all | solution.py:43
  1310.9 17.9 %all-to-all-start.35 = ((f32[4,32,4,512]{3,1,2,0:T(8,128)}), f32[4,32,4,512]{3,1,2,0:T(8,128)S(1)}, u32[]{:S(2)}, u32[]{:S(2)}) async-start(f32[4,32,4,512]{3,1,2,0:T(8,128)} %bitcast.464), calls=%async_computation.35 | async-start | bytes 2097152 | tf_op jit(solution)/shard_map/all_to_all | solution.py:43
  1369.0 98.0 %collective-permute-start.5 = (f32[1,2,32,4,128]{4,2,3,1,0:T(8,128)S(1)}, f32[1,2,32,4,128]{4,2,3,1,0:T(8,128)S(1)}, u32[]{:S(2)}, u32[]{:S(2)}) collective-permute-start(f32[1,2,32,4,128]{4,2,3,1,0:T(8,128)S(1)} %fusion.66), channel_id=1, source_target_pairs={{1,0},{2,1},{3,2},{5,4},{6,5},{7,6},{9,8},{10,9},{11,10},{13,12},{... | collective-permute-start | bytes 393224 | tf_op jit(solution)/shard_map/ppermute | solution.py:55
  1370.3 96.7 %collective-permute-start.4 = (f32[1,2,32,4,128]{4,2,3,1,0:T(8,128)S(1)}, f32[1,2,32,4,128]{4,2,3,1,0:T(8,128)S(1)}, u32[]{:S(2)}, u32[]{:S(2)}) collective-permute-start(f32[1,2,32,4,128]{4,2,3,1,0:T(8,128)S(1)} %fusion.66), channel_id=1, source_target_pairs={{0,1},{1,2},{2,3},{4,5},{5,6},{6,7},{8,9},{9,10},{10,11},{12,13},{... | collective-permute-start | bytes 393224 | tf_op jit(solution)/shard_map/ppermute | solution.py:54
  (51 other events, 4360.6 us)
where the time goes:
time: 1480 us; the launch traced here: 1470 us
  blocking collectives  735 us (50%)
  matrix products  322 us (22%)
  waiting for transfers between devices  169 us (11%)
  starting transfers between devices  126 us (9%)
  local copies, waits for them, and re-layouts  80.7 us (5%)
  other arithmetic  36.6 us (2%)
    psum x75, blocking collectives, by_axis(): return functools.reduce(lax.psum, axes, value)  487 us
    dot_general x9, matrix products, adjoint(): jnp.dot(rows_bf.reshape(batch, scen_local * rows), tech_flat, preferred_e...  152 us
    all_to_all x12, waiting for transfers between devices, sum_at_owner(): lax.all_to_all(blocks, axis, split_axis=0, concat_axis=0, tiled=True)  109 us
    all_to_all x6, blocking collectives, sum_at_owner(): lax.all_to_all(blocks, axis, split_axis=0, concat_axis=0, tiled=True)  101 us
    dot_general x9, matrix products, body(): lax.dot_general(dir_first_bf, tech_flat, (((1,), (1,)), ((), ())), prefer...  96.9 us
    all_gather x1, blocking collectives, body(): first_out = lax.all_gather(first_sol, SCEN, axis=1, tiled=True)  91 us
    all_to_all x12, starting transfers between devices, sum_at_owner(): lax.all_to_all(blocks, axis, split_axis=0, concat_axis=0, tiled=True)  60 us
    all_to_all x14, waiting for transfers between devices, copy_for_each(): lax.all_to_all(jnp.broadcast_to(value[None], (count, *value.shape)), axis...  57.8 us
  transfers between devices with their start and end apart: 32, of which 21 were waited for; matrix products, arithmetic and copies ran while one was open for 4% of the time, Pallas kernels for 0%

commit v1 on v0

v1 whole, which is shorter than its diff:
```python
import functools

import jax
import jax.numpy as jnp
from jax import lax
from jax.experimental import pallas as pl
from jax.experimental.pallas import tpu as pltpu
from jax.sharding import PartitionSpec as P

F32 = jnp.float32
BF16 = jnp.bfloat16
MESH = pl.DeviceIdType.MESH
NS = 32
NC = 4
BATCH = 32
ITERS = 3
CG_STEPS = 3
NCONE = 128
R = 1024
CH = 4


def dot(a, b):
    return jnp.dot(a, b, preferred_element_type=F32)


def dot_nt(a, b):
    return lax.dot_general(a, b, (((1,), (1,)), ((), ())), preferred_element_type=F32)


def two_parts(v):
    high = v.astype(BF16)
    return high, (v - high.astype(F32)).astype(BF16)


def fold(v):
    total = v[:, 0:128]
    for c in range(128, v.shape[1], 128):
        total = total + v[:, c : c + 128]
    return total


def kernel(
    tech, recourse, rhs, cost_first, cost_second, cone,
    first_out, second_out, slack_out, dual_out,
    T, W, rhs_v, image, dual, slack, q, own, pps, ppr, zs, zr, vown, vpart, bx, lx,
    onehot, starts, rx, dx, x, ry, dy, y, by, ly, rs_send, rs_recv, ag, xg, curv_all, norm_all,
    curv_col, norm_col, nres, alpha, beta, sq, sq_dir, fin,
    load_t, load_w, load_r, d2d_v, d2d_p, zsem, scen_sem, col_sem, fin_sem,
):
    me = lax.axis_index("scen")
    col = lax.axis_index("col")
    core = lax.rem(col, 2)
    partner = col + 1 - 2 * core
    across = lax.rem(col + 2, NC)
    bg = me // 8
    cg = lax.rem(me, 8)
    rows8 = pl.ds(pl.multiple_of(bg * 8, 8), 8)

    for i in range(CH):
        for half in range(2):
            scen = (core if half == 0 else 1 - core) * 2 + i // 2
            part = pl.ds((i % 2) * R, R)
            pltpu.make_async_copy(
                tech.at[scen, part], T.at[half * CH + i], load_t.at[half * CH + i]
            ).start()
        pltpu.make_async_copy(
            rhs.at[core * 2 + i // 2, :, pl.ds((i % 2) * R, R)], rhs_v.at[i], load_r.at[i]
        ).start()
    for i in range(CH):
        for half in range(2):
            scen = (core if half == 0 else 1 - core) * 2 + i // 2
            part = pl.ds((i % 2) * R, R)
            pltpu.make_async_copy(
                recourse.at[scen, part], W.at[half * CH + i], load_w.at[half * CH + i]
            ).start()

    barrier = pltpu.get_barrier_semaphore()
    for d in range(1, NS):
        pl.semaphore_signal(
            barrier, inc=1, device_id={"scen": lax.rem(me + d, NS)}, device_id_type=MESH
        )
    for d in range(1, NC):
        pl.semaphore_signal(
            barrier, inc=1, device_id={"col": lax.rem(col + d, NC)}, device_id_type=MESH
        )

    sub = lax.broadcasted_iota(jnp.int32, (BATCH, 128), 0)
    lane = lax.broadcasted_iota(jnp.int32, (BATCH, 128), 1)
    diag = sub == lane

    def to_row(v):
        column = jnp.sum(v, axis=1, keepdims=True)
        return jnp.sum(jnp.where(diag, column, 0.0), axis=0, keepdims=True)

    def to_columns(row):
        picked = jnp.where(diag, jnp.broadcast_to(row, (BATCH, 128)), 0.0)
        return jnp.broadcast_to(jnp.sum(picked, axis=1, keepdims=True), (BATCH, 128))

    def wide(v, n):
        return jnp.concatenate([v] * n, axis=1)

    def set_costs():
        rx[...] = -jnp.broadcast_to(cost_first[cg], (8, 128))
        dx[...] = jnp.zeros((8, 128), F32)
        for j in range(4):
            scen = (core if j < 2 else 1 - core) * 2 + j % 2
            ry[j] = -jnp.broadcast_to(cost_second[scen], (BATCH, 256))
            dy[j] = jnp.zeros((BATCH, 256), F32)

    for i in range(CH):
        image[i] = jnp.zeros((BATCH, R), F32)
        dual[i] = jnp.zeros((BATCH, R), F32)
        slack[i] = jnp.zeros((BATCH, R), F32)
        q[i] = jnp.zeros((BATCH, R), F32)
    x[...] = jnp.zeros((8, 128), F32)
    for j in range(4):
        y[j] = jnp.zeros((BATCH, 256), F32)
    nres[...] = jnp.ones((1, 128), F32)
    beta[...] = jnp.zeros((BATCH, 128), F32)
    set_costs()
    labels = lax.broadcasted_iota(jnp.int32, (NCONE, R), 0)
    row_lane = lax.broadcasted_iota(jnp.int32, (1, 2 * R), 1)
    for j in range(2):
        ids = cone[core * 2 + j]
        before = pltpu.roll(ids, 1, 1)
        fresh = jnp.where((row_lane == 0) | (ids != before), 1.0, 0.0)
        for p in range(2):
            starts[2 * j + p] = fresh[:, p * R : (p + 1) * R]
            here = ids[:, p * R : (p + 1) * R]
            onehot[2 * j + p] = jnp.where(
                jnp.broadcast_to(here, (NCONE, R)) == labels, 1.0, 0.0
            ).astype(BF16)

    for i in range(CH):
        pltpu.make_async_copy(rhs_v.at[i], rhs_v.at[i], load_r.at[i]).wait()
    pl.semaphore_wait(barrier, NS - 1 + NC - 1)

    def to_scens(source, target, sems):
        for d in range(1, NS):
            p = lax.rem(me + d, NS)
            pltpu.make_async_remote_copy(
                source(p), target.at[me], scen_sem.at[sems], scen_sem.at[sems + 1],
                device_id={"scen": p}, device_id_type=MESH,
            ).start()

    def all_came(buffer, sem):
        others = buffer.at[pl.ds(0, buffer.shape[0] - 1)]
        pltpu.make_async_copy(others, others, sem).wait()

    def to_cols(buffer, sems):
        for d in range(1, NC):
            p = lax.rem(col + d, NC)
            pltpu.make_async_remote_copy(
                buffer.at[col], buffer.at[col], col_sem.at[sems], col_sem.at[sems + 1],
                device_id={"col": p}, device_id_type=MESH,
            ).start()

    def rows_copy(i):
        return pltpu.make_async_remote_copy(
            vown.at[i], vpart.at[i], d2d_v.at[0, i], d2d_v.at[1, i],
            device_id={"col": partner}, device_id_type=MESH,
        )

    def partial_copy(i):
        return pltpu.make_async_remote_copy(
            pps.at[i], ppr.at[i], d2d_p.at[0, i], d2d_p.at[1, i],
            device_id={"col": partner}, device_id_type=MESH,
        )

    def across_copy(i):
        return pltpu.make_async_remote_copy(
            zs.at[i], zr.at[i], zsem.at[0, i], zsem.at[1, i],
            device_id={"col": across}, device_id_type=MESH,
        )

    def next_image_step(i):
        across_copy(i).wait()
        step = own[i] + zr[i].astype(F32) + wide(beta[...], R // 128) * q[i]
        q[i] = step
        sq[...] += fold(step * step)
        return step

    def curv_to_cols():
        curv_col[col] = to_row(0.5 * sq[...] + sq_dir[...])
        to_cols(curv_col, 0)

    def curv_to_scens():
        all_came(curv_col, col_sem.at[1])
        all_came(curv_col, col_sem.at[0])
        curv_all[me] = jnp.sum(curv_col[...], axis=0)
        to_scens(lambda p: curv_all.at[me], curv_all, 2)

    def set_alpha():
        all_came(curv_all, scen_sem.at[3])
        all_came(curv_all, scen_sem.at[2])
        alpha[...] = to_columns(nres[...] / jnp.sum(curv_all[...], axis=0))

    def add_steps():
        a = alpha[...]
        x[...] += alpha[rows8, :] * dx[...]
        for j in range(4):
            y[j] += wide(a, 2) * dy[j]
        for i in range(CH):
            image[i] += wide(a, R // 128) * q[i]

    def project():
        for j in range(2):
            sums = jnp.zeros((4 * BATCH, NCONE), F32)
            for i in (2 * j, 2 * j + 1):
                values = rhs_v[i] - image[i] - dual[i]
                start = jnp.broadcast_to(starts[i], (BATCH, R))
                lead_high, lead_low = two_parts(values * start)
                tail_high, tail_low = two_parts(values * values * (1.0 - start))
                stacked = jnp.concatenate([lead_high, lead_low, tail_high, tail_low], axis=0)
                sums = sums + dot_nt(stacked, onehot[i])
            lead = sums[0:32] + sums[32:64]
            norm_tail = jnp.sqrt(jnp.maximum(sums[64:96] + sums[96:128], 0.0))
            inside = norm_tail <= lead
            polar = norm_tail <= -lead
            safe = jnp.where(norm_tail > 0.0, norm_tail, 1.0)
            middle = 0.5 * (lead + norm_tail)
            head = jnp.where(inside, lead, jnp.where(polar, 0.0, middle))
            scale = jnp.where(inside, 1.0, jnp.where(polar, 0.0, middle / safe))
            factors = jnp.concatenate([*two_parts(head), *two_parts(scale)], axis=0)
            for i in (2 * j, 2 * j + 1):
                values = rhs_v[i] - image[i] - dual[i]
                start = jnp.broadcast_to(starts[i], (BATCH, R))
                spread = dot(factors, onehot[i])
                kept = values * (spread[64:96] + spread[96:128])
                new = jnp.where(start > 0.5, spread[0:32] + spread[32:64], kept)
                slack[i] = new
                dual[i] = dual[i] + image[i] + new - rhs_v[i]

    def iteration(t, carry):
        k = lax.rem(t, CG_STEPS)
        first = k == 0
        sq[...] = jnp.zeros((BATCH, 128), F32)

        def theirs(i):
            rows_copy(i).wait_recv()

            @pl.when(t == 0)
            def _():
                pltpu.make_async_copy(T.at[CH + i], T.at[CH + i], load_t.at[CH + i]).wait()

            return dot(vpart[i], T[CH + i])

        for i in range(CH):

            @pl.when(first)
            def _(i=i):
                vown[i] = (rhs_v[i] - slack[i] - dual[i] - image[i]).astype(BF16)

            @pl.when(jnp.logical_not(first))
            def _(i=i):
                vown[i] = next_image_step(i).astype(BF16)

            rows_copy(i).start()

            @pl.when(t == 0)
            def _(i=i):
                pltpu.make_async_copy(T.at[i], T.at[i], load_t.at[i]).wait()

            if i == 0:
                bx[...] = dot(vown[i], T[i])
            else:
                bx[...] += dot(vown[i], T[i])
                bx[...] += theirs(i - 1)

        @pl.when(jnp.logical_not(first))
        def _():
            curv_to_cols()

        total = bx[...] + theirs(CH - 1)
        for b in range(4):
            for c in range(8):
                rs_send[b * 8 + c] = total[b * 8 : b * 8 + 8, c * 128 : c * 128 + 128]
        to_scens(lambda p: rs_send.at[p], rs_recv, 0)
        rs_recv[me] = rs_send[me]

        @pl.when(jnp.logical_not(first))
        def _():
            curv_to_scens()

        @pl.when(t == 0)
        def _():
            for i in range(2 * CH):
                pltpu.make_async_copy(W.at[i], W.at[i], load_w.at[i]).wait()

        for j in range(4):
            rows = vown if j < 2 else vpart
            a = 2 * (j % 2)
            by[j] = dot(rows[a], W[2 * j]) + dot(rows[a + 1], W[2 * j + 1])

        @pl.when(first)
        def _():
            alpha[...] = jnp.full((BATCH, 128), -1.0, F32)

        @pl.when(jnp.logical_not(first))
        def _():
            set_alpha()

        all_came(rs_recv, scen_sem.at[1])
        back = jnp.sum(rs_recv[...], axis=0)
        res = rx[...] - alpha[rows8, :] * (dx[...] + back)
        rx[...] = res
        ag[me] = res.astype(BF16)
        to_scens(lambda p: ag.at[me], ag, 4)
        all_came(rs_send, scen_sem.at[0])

        norm = jnp.zeros((BATCH, 128), F32)
        for j in range(4):
            r = ry[j] - wide(alpha[...], 2) * (dy[j] + by[j])
            ry[j] = r
            ly[j] = r.astype(BF16)
            norm = norm + fold(r * r)
        sq_dir[...] = norm
        sq_dir[rows8, :] += res * res
        norm_all[me] = to_row(sq_dir[...])
        to_scens(lambda p: norm_all.at[me], norm_all, 6)
        add_steps()
        for i in range(CH):
            rows_copy(i).wait_send()
        all_came(norm_all, scen_sem.at[7])
        all_came(norm_all, scen_sem.at[6])
        norm_col[col] = jnp.sum(norm_all[...], axis=0)
        to_cols(norm_col, 2)
        all_came(ag, scen_sem.at[5])
        all_came(ag, scen_sem.at[4])
        for b in range(4):
            for c in range(8):
                xg[b * 8 : b * 8 + 8, c * 128 : c * 128 + 128] = ag[b * 8 + c].astype(F32)
        lx[...] = xg[...].astype(BF16)

        def exchange(i):
            partial_copy(i).wait_recv()
            here = own[i] + ppr[i]
            own[i] = here
            zs[i] = here.astype(BF16)
            across_copy(i).start()

        for i in range(CH):
            pps[i] = dot_nt(lx[...], T[CH + i]) + dot_nt(ly[2 + i // 2], W[CH + i])
            partial_copy(i).start()
            own[i] = dot_nt(lx[...], T[i]) + dot_nt(ly[i // 2], W[i])
            if i:
                exchange(i - 1)
        exchange(CH - 1)

        all_came(norm_col, col_sem.at[3])
        all_came(norm_col, col_sem.at[2])
        new_norm = jnp.sum(norm_col[...], axis=0)

        @pl.when(first)
        def _():
            beta[...] = jnp.zeros((BATCH, 128), F32)
            for i in range(CH):
                q[i] = jnp.zeros((BATCH, R), F32)

        @pl.when(jnp.logical_not(first))
        def _():
            beta[...] = to_columns(new_norm / nres[...])

        nres[...] = new_norm
        norm = jnp.zeros((BATCH, 128), F32)
        for j in range(4):
            d = ry[j] + wide(beta[...], 2) * dy[j]
            dy[j] = d
            norm = norm + fold(d * d)
        sq_dir[...] = norm
        d = rx[...] + beta[rows8, :] * dx[...]
        dx[...] = d
        sq_dir[rows8, :] += d * d
        for i in range(CH):
            partial_copy(i).wait_send()

        @pl.when(k == CG_STEPS - 1)
        def _():
            sq[...] = jnp.zeros((BATCH, 128), F32)
            for i in range(CH):
                next_image_step(i)
            curv_to_cols()
            curv_to_scens()
            set_alpha()
            add_steps()

            @pl.when(t == ITERS * CG_STEPS - 1)
            def _():
                rs_recv[me] = x[...]
                to_scens(lambda p: rs_recv.at[me], rs_recv, 0)

            set_costs()
            for i in range(CH):
                q[i] = jnp.zeros((BATCH, R), F32)
            project()

        return carry

    lax.fori_loop(0, ITERS * CG_STEPS, iteration, 0)

    quarter = col // 2
    lanes_here = pl.ds(pl.multiple_of(core * 512, 128), 512)
    lanes_there = pl.ds(pl.multiple_of((1 - core) * 512, 128), 512)

    def last_copy(a, j):
        return pltpu.make_async_remote_copy(
            (slack, dual)[a].at[2 * j + quarter, :, lanes_there], fin.at[a, j],
            fin_sem.at[0, a, j], fin_sem.at[1, a, j],
            device_id={"col": partner}, device_id_type=MESH,
        )

    for a in range(2):
        for j in range(2):
            last_copy(a, j).start()
    for j in range(2):
        slack_out[core * 2 + j] = slack[2 * j + quarter, :, lanes_here]
        dual_out[core * 2 + j] = dual[2 * j + quarter, :, lanes_here]
        second_out[core * 2 + j] = y[j]
        second_out[(1 - core) * 2 + j] = y[2 + j]
    for a in range(2):
        for j in range(2):
            last_copy(a, j).wait()
            (slack_out, dual_out)[a][(1 - core) * 2 + j] = fin[a, j]
    all_came(rs_recv, scen_sem.at[1])
    all_came(rs_recv, scen_sem.at[0])
    for b in range(4):
        for c in range(8):
            first_out[b * 8 : b * 8 + 8, c * 128 : c * 128 + 128] = rs_recv[b * 8 + c]


def body(tech, recourse, rhs, cost_first, cost_second, cone_id):
    any_space = pl.BlockSpec(memory_space=pl.ANY)
    vmem = pl.BlockSpec(memory_space=pltpu.VMEM)
    rows_f32 = pltpu.VMEM((CH, BATCH, R), F32)
    rows_bf16 = pltpu.VMEM((CH, BATCH, R), BF16)
    block = pltpu.VMEM((8, 128), F32)
    ys = pltpu.VMEM((4, BATCH, 256), F32)
    dma = pltpu.SemaphoreType.DMA
    first, second, slack, dual = pl.pallas_call(
        kernel,
        out_shape=(
            jax.ShapeDtypeStruct((BATCH, 1024), F32),
            jax.ShapeDtypeStruct((4, BATCH, 256), F32),
            jax.ShapeDtypeStruct((4, BATCH, 512), F32),
            jax.ShapeDtypeStruct((4, BATCH, 512), F32),
        ),
        in_specs=[any_space, any_space, any_space, vmem, vmem, vmem],
        out_specs=(vmem, vmem, vmem, vmem),
        scratch_shapes=[
            pltpu.VMEM((2 * CH, R, 1024), BF16),
            pltpu.VMEM((2 * CH, R, 256), BF16),
            rows_f32, rows_f32, rows_f32, rows_f32, rows_f32,
            rows_f32, rows_f32, rows_f32,
            rows_bf16, rows_bf16, rows_bf16, rows_bf16,
            pltpu.VMEM((BATCH, 1024), F32),
            pltpu.VMEM((BATCH, 1024), BF16),
            pltpu.VMEM((CH, NCONE, R), BF16),
            pltpu.VMEM((CH, 1, R), F32),
            block, block, block,
            ys, ys, ys, ys,
            pltpu.VMEM((4, BATCH, 256), BF16),
            pltpu.VMEM((NS, 8, 128), F32),
            pltpu.VMEM((NS, 8, 128), F32),
            pltpu.VMEM((NS, 8, 128), BF16),
            pltpu.VMEM((BATCH, 1024), F32),
            pltpu.VMEM((NS, 1, 128), F32),
            pltpu.VMEM((NS, 1, 128), F32),
            pltpu.VMEM((NC, 1, 128), F32),
            pltpu.VMEM((NC, 1, 128), F32),
            pltpu.VMEM((1, 128), F32),
            pltpu.VMEM((BATCH, 128), F32),
            pltpu.VMEM((BATCH, 128), F32),
            pltpu.VMEM((BATCH, 128), F32),
            pltpu.VMEM((BATCH, 128), F32),
            pltpu.VMEM((2, 2, BATCH, 512), F32),
            dma((2 * CH,)), dma((2 * CH,)), dma((CH,)),
            dma((2, CH)), dma((2, CH)), dma((2, CH)),
            dma((8,)), dma((4,)), dma((2, 2, 2)),
        ],
        compiler_params=pltpu.CompilerParams(
            collective_id=0, has_side_effects=True, vmem_limit_bytes=60 * 2**20
        ),
    )(
        tech,
        recourse,
        jnp.transpose(rhs, (1, 0, 2)),
        cost_first.reshape(8, 1, 128),
        cost_second.reshape(4, 1, 256),
        cone_id.reshape(4, 1, 2048),
    )
    return (
        first,
        jnp.transpose(second, (1, 0, 2)),
        jnp.transpose(slack, (1, 0, 2)),
        jnp.transpose(dual, (1, 0, 2)),
    )


def solution(mesh):
    return jax.shard_map(
        body,
        mesh=mesh,
        in_specs=(
            P("scen", None, "col"),
            P("scen", None, "col"),
            P(None, "scen", None),
            P("col"),
            P("scen", "col"),
            P("scen", None),
        ),
        out_specs=(
            P(None, "col"),
            P(None, "scen", "col"),
            P(None, "scen", "col"),
            P(None, "scen", "col"),
        ),
        check_vma=False,
    )
```

time: 1480 us -> 305 us (0.21)
  blocking collectives: 735 us -> 0 us
  matrix products: 322 us -> 0 us
  Pallas kernels: 0 us -> 291 us
  waiting for transfers between devices: 169 us -> 0 us
  starting transfers between devices: 126 us -> 0 us
  local copies, waits for them, and re-layouts: 80.7 us -> 12.4 us
  other arithmetic: 36.6 us -> 0 us
    psum x75 -> x0, blocking collectives: 487 us -> none  [by_axis(): return functools.reduce(lax.psum, axes, value)]
    dot_general x48 -> x0, matrix products: 322 us -> none  [the longest x9 152 us: adjoint(): jnp.dot(rows_bf.reshape(batch, scen_local * rows), tech_flat, preferred_e...]
    pallas_call x0 -> x1, Pallas kernels: none -> 291 us  [body(): pl.pallas_call(kernel, out_shape=(jax.ShapeDtypeStruct((BATCH, 1024), F32...]
    all_to_all x26 -> x0, waiting for transfers between devices: 167 us -> none  [the longest x12 109 us: sum_at_owner(): lax.all_to_all(blocks, axis, split_axis=0, concat_axis=0, tiled=True)]
    all_to_all x10 -> x0, blocking collectives: 156 us -> none  [the longest x6 101 us: sum_at_owner(): lax.all_to_all(blocks, axis, split_axis=0, concat_axis=0, tiled=True)]
    all_to_all x26 -> x0, starting transfers between devices: 113 us -> none  [the longest x12 60 us: sum_at_owner(): lax.all_to_all(blocks, axis, split_axis=0, concat_axis=0, tiled=True)]
    all_gather x1 -> x0, blocking collectives: 91 us -> none  [body(): first_out = lax.all_gather(first_sol, SCEN, axis=1, tiled=True)]
    dot_general x1 -> x0, local copies, waits for them, and re-layouts: 20.9 us -> none  [adjoint(): jnp.dot(rows_bf.reshape(batch, scen_local * rows), tech_flat, preferred_e...]
  transfers between devices with their start and end apart: 32 -> 0, of which waited for: 21 -> 0; matrix products, arithmetic and copies ran while one was open for 4% -> 0% of each run, Pallas kernels for 0% -> 0%
where the time goes in v1:
time: 305 us; the launch traced here: 304 us
  Pallas kernels  291 us (95%)
  local copies, waits for them, and re-layouts  12.4 us (4%)
    pallas_call x1, Pallas kernels, body(): pl.pallas_call(kernel, out_shape=(jax.ShapeDtypeStruct((BATCH, 1024), F32...  291 us
    unnamed x5, local copies, waits for them, and re-layouts  9.68 us

profile of v1, /device:TPU:0, one launch (start us, length us, event | category | flops | bytes accessed | tf_op | source)
XLA Modules:
  0.0 304.3 jit_solution(17120279876212367280)
XLA Ops:
  0.6 1.3 reshape.18.cost_second
  1.9 1.4 reshape.19.cone
  3.3 2.8 copy.15
  6.1 291.3 %shard_map.93 = (f32[32,1024]{1,0:T(8,128)}, f32[4,32,256]{2,1,0:T(8,128)}, f32[4,32,512]{2,1,0:T(8,128)}, f32[4,32,512]{2,1,0:T(8,128)}) custom-call(bf16[4,2048,1024]{2,1,0:T(8,128)(2,1)} %tech.1, bf16[4,2048,256]{2,1,0:T(8,128)(2,1)} %recourse.1, f32[4,32,2048]{2,1,0:T(8,128)} %bitcast.7, f32[8,1,128]{2,1,0:T(1,128)} %bitcast.11, ...), custom_call_target="tpu_custom_call" | custom-call | tf_op jit(solution)/shard_map/pallas_call | solution.py:440
  297.5 1.6 copy.11
  299.1 1.8 copy.12
  300.9 1.8 copy.13
  302.8 1.6 copy.17

commit v2 on v1

--- a/solution.py
+++ b/solution.py
@@ -11,6 +11,7 @@
 BF16 = jnp.bfloat16
 MESH = pl.DeviceIdType.MESH
 NS = 32
+NP = 16
 NC = 4
 BATCH = 32
 ITERS = 3
@@ -43,19 +44,20 @@
 def kernel(
     tech, recourse, rhs, cost_first, cost_second, cone,
     first_out, second_out, slack_out, dual_out,
-    T, W, rhs_v, image, dual, slack, q, own, pps, ppr, zs, zr, vown, vpart, bx, lx,
+    T, W, TT, WT, rhs_v, image, dual, slack, q, own, pps, ppr, zs, zr, vown, vpart, bx, lx,
     onehot, starts, rx, dx, x, ry, dy, y, by, ly, rs_send, rs_recv, ag, xg, curv_all, norm_all,
-    curv_col, norm_col, nres, alpha, beta, sq, sq_dir, fin,
-    load_t, load_w, load_r, d2d_v, d2d_p, zsem, scen_sem, col_sem, fin_sem,
+    q_row, dir_col, norm_col, nres, alpha, beta, sq, sq_dir, fin,
+    load_t, load_w, load_r, d2d_v, d2d_p, zsem, scen_sem, col_sem, row_sem, fin_sem,
 ):
     me = lax.axis_index("scen")
     col = lax.axis_index("col")
     core = lax.rem(col, 2)
     partner = col + 1 - 2 * core
     across = lax.rem(col + 2, NC)
-    bg = me // 8
-    cg = lax.rem(me, 8)
-    rows8 = pl.ds(pl.multiple_of(bg * 8, 8), 8)
+    plane = me // NP
+    place = lax.rem(me, NP)
+    cg = lax.rem(place, 8)
+    rows16 = pl.ds(pl.multiple_of((place // 8) * 16, 16), 16)
 
     for i in range(CH):
         for half in range(2):
@@ -65,7 +67,7 @@
                 tech.at[scen, part], T.at[half * CH + i], load_t.at[half * CH + i]
             ).start()
         pltpu.make_async_copy(
-            rhs.at[core * 2 + i // 2, :, pl.ds((i % 2) * R, R)], rhs_v.at[i], load_r.at[i]
+            rhs.at[:, core * 2 + i // 2, pl.ds((i % 2) * R, R)], rhs_v.at[i], load_r.at[i]
         ).start()
     for i in range(CH):
         for half in range(2):
@@ -100,12 +102,15 @@
     def wide(v, n):
         return jnp.concatenate([v] * n, axis=1)
 
+    def pick(ref, half, j):
+        return jnp.where(half == 0, ref[j : j + 1, :], ref[2 + j : 3 + j, :])
+
     def set_costs():
-        rx[...] = -jnp.broadcast_to(cost_first[cg], (8, 128))
-        dx[...] = jnp.zeros((8, 128), F32)
+        rx[...] = -jnp.broadcast_to(cost_first[cg], (16, 128))
+        dx[...] = jnp.zeros((16, 128), F32)
         for j in range(4):
-            scen = (core if j < 2 else 1 - core) * 2 + j % 2
-            ry[j] = -jnp.broadcast_to(cost_second[scen], (BATCH, 256))
+            cost = pick(cost_second, core if j < 2 else 1 - core, j % 2)
+            ry[j] = -jnp.broadcast_to(cost, (BATCH, 256))
             dy[j] = jnp.zeros((BATCH, 256), F32)
 
     for i in range(CH):
@@ -113,7 +118,7 @@
         dual[i] = jnp.zeros((BATCH, R), F32)
         slack[i] = jnp.zeros((BATCH, R), F32)
         q[i] = jnp.zeros((BATCH, R), F32)
-    x[...] = jnp.zeros((8, 128), F32)
+    x[...] = jnp.zeros((16, 128), F32)
     for j in range(4):
         y[j] = jnp.zeros((BATCH, 256), F32)
     nres[...] = jnp.ones((1, 128), F32)
@@ -122,7 +127,7 @@
     labels = lax.broadcasted_iota(jnp.int32, (NCONE, R), 0)
     row_lane = lax.broadcasted_iota(jnp.int32, (1, 2 * R), 1)
     for j in range(2):
-        ids = cone[core * 2 + j]
+        ids = pick(cone, core, j)
         before = pltpu.roll(ids, 1, 1)
         fresh = jnp.where((row_lane == 0) | (ids != before), 1.0, 0.0)
         for p in range(2):
@@ -144,6 +149,14 @@
                 device_id={"scen": p}, device_id_type=MESH,
             ).start()
 
+    def to_plane(buffer, sems):
+        for d in range(1, NP):
+            p = plane * NP + lax.rem(place + d, NP)
+            pltpu.make_async_remote_copy(
+                buffer.at[place], buffer.at[place], scen_sem.at[sems], scen_sem.at[sems + 1],
+                device_id={"scen": p}, device_id_type=MESH,
+            ).start()
+
     def all_came(buffer, sem):
         others = buffer.at[pl.ds(0, buffer.shape[0] - 1)]
         pltpu.make_async_copy(others, others, sem).wait()
@@ -168,27 +181,34 @@
             device_id={"col": partner}, device_id_type=MESH,
         )
 
-    def across_copy(i):
+    def across_copy(i, turn):
         return pltpu.make_async_remote_copy(
-            zs.at[i], zr.at[i], zsem.at[0, i], zsem.at[1, i],
+            zs.at[i], zr.at[turn, i], zsem.at[0, i], zsem.at[1 + turn, i],
             device_id={"col": across}, device_id_type=MESH,
         )
 
-    def next_image_step(i):
-        across_copy(i).wait()
-        step = own[i] + zr[i].astype(F32) + wide(beta[...], R // 128) * q[i]
+    def next_image_step(i, turn):
+        across_copy(i, turn).wait()
+        step = own[i] + zr[turn, i].astype(F32) + wide(beta[...], R // 128) * q[i]
         q[i] = step
         sq[...] += fold(step * step)
         return step
 
-    def curv_to_cols():
-        curv_col[col] = to_row(0.5 * sq[...] + sq_dir[...])
-        to_cols(curv_col, 0)
+    def row_copy():
+        return pltpu.make_async_remote_copy(
+            q_row.at[core], q_row.at[core], row_sem.at[0], row_sem.at[1],
+            device_id={"col": partner}, device_id_type=MESH,
+        )
+
+    def curv_to_partner():
+        q_row[core] = to_row(sq[...])
+        row_copy().start()
 
     def curv_to_scens():
-        all_came(curv_col, col_sem.at[1])
-        all_came(curv_col, col_sem.at[0])
-        curv_all[me] = jnp.sum(curv_col[...], axis=0)
+        all_came(dir_col, col_sem.at[1])
+        all_came(dir_col, col_sem.at[0])
+        row_copy().wait()
+        curv_all[me] = jnp.sum(dir_col[...], axis=0) + jnp.sum(q_row[...], axis=0)
         to_scens(lambda p: curv_all.at[me], curv_all, 2)
 
     def set_alpha():
@@ -198,7 +218,7 @@
 
     def add_steps():
         a = alpha[...]
-        x[...] += alpha[rows8, :] * dx[...]
+        x[...] += alpha[rows16, :] * dx[...]
         for j in range(4):
             y[j] += wide(a, 2) * dy[j]
         for i in range(CH):
@@ -235,6 +255,7 @@
     def iteration(t, carry):
         k = lax.rem(t, CG_STEPS)
         first = k == 0
+        turn = lax.rem(t, 2)
         sq[...] = jnp.zeros((BATCH, 128), F32)
 
         def theirs(i):
@@ -254,7 +275,7 @@
 
             @pl.when(jnp.logical_not(first))
             def _(i=i):
-                vown[i] = next_image_step(i).astype(BF16)
+                vown[i] = next_image_step(i, 1 - turn).astype(BF16)
 
             rows_copy(i).start()
 
@@ -270,14 +291,15 @@
 
         @pl.when(jnp.logical_not(first))
         def _():
-            curv_to_cols()
+            curv_to_partner()
 
         total = bx[...] + theirs(CH - 1)
-        for b in range(4):
+        for b in range(2):
             for c in range(8):
-                rs_send[b * 8 + c] = total[b * 8 : b * 8 + 8, c * 128 : c * 128 + 128]
-        to_scens(lambda p: rs_send.at[p], rs_recv, 0)
-        rs_recv[me] = rs_send[me]
+                tile = total[b * 16 : b * 16 + 16, c * 128 : c * 128 + 128]
+                rs_send[b * 8 + c] = tile.astype(BF16)
+        to_scens(lambda p: rs_send.at[lax.rem(p, NP)], rs_recv, 0)
+        rs_recv[me] = rs_send[place]
 
         @pl.when(jnp.logical_not(first))
         def _():
@@ -287,6 +309,15 @@
         def _():
             for i in range(2 * CH):
                 pltpu.make_async_copy(W.at[i], W.at[i], load_w.at[i]).wait()
+
+            def turned(i, carry):
+                for b in range(0, R, 256):
+                    for c in range(0, 1024, 256):
+                        TT[i, c : c + 256, b : b + 256] = T[i, b : b + 256, c : c + 256].T
+                    WT[i, :, b : b + 256] = W[i, b : b + 256, :].T
+                return carry
+
+            lax.fori_loop(0, 2 * CH, turned, 0)
 
         for j in range(4):
             rows = vown if j < 2 else vpart
@@ -302,12 +333,12 @@
             set_alpha()
 
         all_came(rs_recv, scen_sem.at[1])
-        back = jnp.sum(rs_recv[...], axis=0)
-        res = rx[...] - alpha[rows8, :] * (dx[...] + back)
+        back = jnp.sum(rs_recv[...].astype(F32), axis=0)
+        res = rx[...] - alpha[rows16, :] * (dx[...] + back)
         rx[...] = res
-        ag[me] = res.astype(BF16)
-        to_scens(lambda p: ag.at[me], ag, 4)
-        all_came(rs_send, scen_sem.at[0])
+        ag[place] = res.astype(BF16)
+        to_plane(ag, 4)
+        all_came(rs_recv, scen_sem.at[0])
 
         norm = jnp.zeros((BATCH, 128), F32)
         for j in range(4):
@@ -316,36 +347,39 @@
             ly[j] = r.astype(BF16)
             norm = norm + fold(r * r)
         sq_dir[...] = norm
-        sq_dir[rows8, :] += res * res
+        sq_dir[rows16, :] += 0.5 * (res * res)
         norm_all[me] = to_row(sq_dir[...])
         to_scens(lambda p: norm_all.at[me], norm_all, 6)
         add_steps()
         for i in range(CH):
             rows_copy(i).wait_send()
-        all_came(norm_all, scen_sem.at[7])
-        all_came(norm_all, scen_sem.at[6])
-        norm_col[col] = jnp.sum(norm_all[...], axis=0)
-        to_cols(norm_col, 2)
+        for i in range(CH):
+            pps[i] = dot(ly[2 + i // 2], WT[CH + i])
+            own[i] = dot(ly[i // 2], WT[i])
         all_came(ag, scen_sem.at[5])
         all_came(ag, scen_sem.at[4])
-        for b in range(4):
+        for b in range(2):
             for c in range(8):
-                xg[b * 8 : b * 8 + 8, c * 128 : c * 128 + 128] = ag[b * 8 + c].astype(F32)
-        lx[...] = xg[...].astype(BF16)
+                lx[b * 16 : b * 16 + 16, c * 128 : c * 128 + 128] = ag[b * 8 + c]
 
         def exchange(i):
             partial_copy(i).wait_recv()
             here = own[i] + ppr[i]
             own[i] = here
             zs[i] = here.astype(BF16)
-            across_copy(i).start()
+            across_copy(i, turn).start()
 
         for i in range(CH):
-            pps[i] = dot_nt(lx[...], T[CH + i]) + dot_nt(ly[2 + i // 2], W[CH + i])
+            pps[i] += dot(lx[...], TT[CH + i])
             partial_copy(i).start()
-            own[i] = dot_nt(lx[...], T[i]) + dot_nt(ly[i // 2], W[i])
+            own[i] += dot(lx[...], TT[i])
             if i:
                 exchange(i - 1)
+            if i == 1:
+                all_came(norm_all, scen_sem.at[7])
+                all_came(norm_all, scen_sem.at[6])
+                norm_col[col] = jnp.sum(norm_all[...], axis=0)
+                to_cols(norm_col, 2)
         exchange(CH - 1)
 
         all_came(norm_col, col_sem.at[3])
@@ -369,9 +403,11 @@
             dy[j] = d
             norm = norm + fold(d * d)
         sq_dir[...] = norm
-        d = rx[...] + beta[rows8, :] * dx[...]
+        d = rx[...] + beta[rows16, :] * dx[...]
         dx[...] = d
-        sq_dir[rows8, :] += d * d
+        sq_dir[rows16, :] += 0.5 * (d * d)
+        dir_col[col] = to_row(sq_dir[...])
+        to_cols(dir_col, 0)
         for i in range(CH):
             partial_copy(i).wait_send()
 
@@ -379,16 +415,16 @@
         def _():
             sq[...] = jnp.zeros((BATCH, 128), F32)
             for i in range(CH):
-                next_image_step(i)
-            curv_to_cols()
+                next_image_step(i, turn)
+            curv_to_partner()
             curv_to_scens()
             set_alpha()
             add_steps()
 
             @pl.when(t == ITERS * CG_STEPS - 1)
             def _():
-                rs_recv[me] = x[...]
-                to_scens(lambda p: rs_recv.at[me], rs_recv, 0)
+                xg[place] = x[...]
+                to_plane(xg, 8)
 
             set_costs()
             for i in range(CH):
@@ -422,11 +458,19 @@
         for j in range(2):
             last_copy(a, j).wait()
             (slack_out, dual_out)[a][(1 - core) * 2 + j] = fin[a, j]
-    all_came(rs_recv, scen_sem.at[1])
-    all_came(rs_recv, scen_sem.at[0])
-    for b in range(4):
+    all_came(xg, scen_sem.at[9])
+    all_came(xg, scen_sem.at[8])
+    for b in range(2):
         for c in range(8):
-            first_out[b * 8 : b * 8 + 8, c * 128 : c * 128 + 128] = rs_recv[b * 8 + c]
+            first_out[b * 16 : b * 16 + 16, c * 128 : c * 128 + 128] = xg[b * 8 + c]
+
+
+def finish(first, second, slack, dual, first_out, second_out, slack_out, dual_out):
+    first_out[...] = first[...]
+    for j in range(4):
+        second_out[:, j, :] = second[j]
+        slack_out[:, j, :] = slack[j]
+        dual_out[:, j, :] = dual[j]
 
 
 def body(tech, recourse, rhs, cost_first, cost_second, cone_id):
@@ -434,7 +478,7 @@
     vmem = pl.BlockSpec(memory_space=pltpu.VMEM)
     rows_f32 = pltpu.VMEM((CH, BATCH, R), F32)
     rows_bf16 = pltpu.VMEM((CH, BATCH, R), BF16)
-    block = pltpu.VMEM((8, 128), F32)
+    block = pltpu.VMEM((16, 128), F32)
     ys = pltpu.VMEM((4, BATCH, 256), F32)
     dma = pltpu.SemaphoreType.DMA
     first, second, slack, dual = pl.pallas_call(
@@ -450,9 +494,12 @@
         scratch_shapes=[
             pltpu.VMEM((2 * CH, R, 1024), BF16),
             pltpu.VMEM((2 * CH, R, 256), BF16),
+            pltpu.VMEM((2 * CH, 1024, R), BF16),
+            pltpu.VMEM((2 * CH, 256, R), BF16),
             rows_f32, rows_f32, rows_f32, rows_f32, rows_f32,
             rows_f32, rows_f32, rows_f32,
-            rows_bf16, rows_bf16, rows_bf16, rows_bf16,
+            rows_bf16, pltpu.VMEM((2, CH, BATCH, R), BF16),
+            rows_bf16, rows_bf16,
             pltpu.VMEM((BATCH, 1024), F32),
             pltpu.VMEM((BATCH, 1024), BF16),
             pltpu.VMEM((CH, NCONE, R), BF16),
@@ -460,12 +507,13 @@
             block, block, block,
             ys, ys, ys, ys,
             pltpu.VMEM((4, BATCH, 256), BF16),
-            pltpu.VMEM((NS, 8, 128), F32),
-            pltpu.VMEM((NS, 8, 128), F32),
-            pltpu.VMEM((NS, 8, 128), BF16),
-            pltpu.VMEM((BATCH, 1024), F32),
+            pltpu.VMEM((NP, 16, 128), BF16),
+            pltpu.VMEM((NS, 16, 128), BF16),
+            pltpu.VMEM((NP, 16, 128), BF16),
+            pltpu.VMEM((NP, 16, 128), F32),
             pltpu.VMEM((NS, 1, 128), F32),
             pltpu.VMEM((NS, 1, 128), F32),
+            pltpu.VMEM((2, 1, 128), F32),
             pltpu.VMEM((NC, 1, 128), F32),
             pltpu.VMEM((NC, 1, 128), F32),
             pltpu.VMEM((1, 128), F32),
@@ -475,8 +523,8 @@
             pltpu.VMEM((BATCH, 128), F32),
             pltpu.VMEM((2, 2, BATCH, 512), F32),
             dma((2 * CH,)), dma((2 * CH,)), dma((CH,)),
-            dma((2, CH)), dma((2, CH)), dma((2, CH)),
-            dma((8,)), dma((4,)), dma((2, 2, 2)),
+            dma((2, CH)), dma((2, CH)), dma((3, CH)),
+            dma((10,)), dma((4,)), dma((2,)), dma((2, 2, 2)),
         ],
         compiler_params=pltpu.CompilerParams(
             collective_id=0, has_side_effects=True, vmem_limit_bytes=60 * 2**20
@@ -484,17 +532,22 @@
     )(
         tech,
         recourse,
-        jnp.transpose(rhs, (1, 0, 2)),
+        rhs,
         cost_first.reshape(8, 1, 128),
-        cost_second.reshape(4, 1, 256),
-        cone_id.reshape(4, 1, 2048),
+        cost_second,
+        cone_id,
     )
-    return (
-        first,
-        jnp.transpose(second, (1, 0, 2)),
-        jnp.transpose(slack, (1, 0, 2)),
-        jnp.transpose(dual, (1, 0, 2)),
-    )
+    return pl.pallas_call(
+        finish,
+        out_shape=(
+            jax.ShapeDtypeStruct((BATCH, 1024), F32),
+            jax.ShapeDtypeStruct((BATCH, 4, 256), F32),
+            jax.ShapeDtypeStruct((BATCH, 4, 512), F32),
+            jax.ShapeDtypeStruct((BATCH, 4, 512), F32),
+        ),
+        in_specs=[vmem, vmem, vmem, vmem],
+        out_specs=(vmem, vmem, vmem, vmem),
+    )(first, second, slack, dual)
 
 
 def solution(mesh):

time: 305 us -> 255 us (0.84)
  Pallas kernels: 291 us -> 254 us
  local copies, waits for them, and re-layouts: 12.4 us -> 0 us
    pallas_call x1, Pallas kernels: 291 us -> 252 us  [body(): pl.pallas_call(kernel, out_shape=(jax.ShapeDtypeStruct((BATCH, 1024), F32...]
    unnamed x5 -> x0, local copies, waits for them, and re-layouts: 9.68 us -> none
where the time goes in v2:
time: 255 us
  Pallas kernels  254 us (100%)
    pallas_call x1, Pallas kernels, body(): pl.pallas_call(kernel, out_shape=(jax.ShapeDtypeStruct((BATCH, 1024), F32...  252 us

profile of v2, /device:TPU:0, one launch (start us, length us, event | category | flops | bytes accessed | tf_op | source)
XLA Modules:
  0.0 255.1 jit_solution(13612858422335478377)
XLA Ops:
  0.6 252.3 %shard_map.93 = (f32[32,1024]{1,0:T(8,128)}, f32[4,32,256]{2,1,0:T(8,128)}, f32[4,32,512]{2,1,0:T(8,128)}, f32[4,32,512]{2,1,0:T(8,128)}) custom-call(bf16[4,2048,1024]{2,1,0:T(8,128)(2,1)} %tech.1, bf16[4,2048,256]{2,1,0:T(8,128)(2,1)} %recourse.1, f32[32,4,2048]{2,1,0:T(4,128)} %rhs.1, f32[8,1,128]{2,1,0:T(1,128)} %bitcast.1, f32[4,256]{1,0:T(4,128)} %cost_second.1, ...), custom_call_target="tpu_custom_call" | custom-call | tf_op jit(solution)/shard_map/pallas_call | solution.py:484
  253.0 2.1 shard_map.94

commit v3 on v2

--- a/solution.py
+++ b/solution.py
@@ -18,7 +18,12 @@
 CG_STEPS = 3
 NCONE = 128
 R = 1024
-CH = 4
+PER = 2048 // R
+CH = 2 * PER
+STEPS = sorted(
+    ((z, x, y) for z in range(2) for x in range(4) for y in range(4) if z + x + y),
+    key=lambda s: -(2 * s[0] + min(s[1], 4 - s[1]) + min(s[2], 4 - s[2])),
+)
 
 
 def dot(a, b):
@@ -61,18 +66,18 @@
 
     for i in range(CH):
         for half in range(2):
-            scen = (core if half == 0 else 1 - core) * 2 + i // 2
-            part = pl.ds((i % 2) * R, R)
+            scen = (core if half == 0 else 1 - core) * 2 + i // PER
+            part = pl.ds((i % PER) * R, R)
             pltpu.make_async_copy(
                 tech.at[scen, part], T.at[half * CH + i], load_t.at[half * CH + i]
             ).start()
         pltpu.make_async_copy(
-            rhs.at[:, core * 2 + i // 2, pl.ds((i % 2) * R, R)], rhs_v.at[i], load_r.at[i]
+            rhs.at[:, core * 2 + i // PER, pl.ds((i % PER) * R, R)], rhs_v.at[i], load_r.at[i]
         ).start()
     for i in range(CH):
         for half in range(2):
-            scen = (core if half == 0 else 1 - core) * 2 + i // 2
-            part = pl.ds((i % 2) * R, R)
+            scen = (core if half == 0 else 1 - core) * 2 + i // PER
+            part = pl.ds((i % PER) * R, R)
             pltpu.make_async_copy(
                 recourse.at[scen, part], W.at[half * CH + i], load_w.at[half * CH + i]
             ).start()
@@ -125,15 +130,15 @@
     beta[...] = jnp.zeros((BATCH, 128), F32)
     set_costs()
     labels = lax.broadcasted_iota(jnp.int32, (NCONE, R), 0)
-    row_lane = lax.broadcasted_iota(jnp.int32, (1, 2 * R), 1)
+    row_lane = lax.broadcasted_iota(jnp.int32, (1, PER * R), 1)
     for j in range(2):
         ids = pick(cone, core, j)
         before = pltpu.roll(ids, 1, 1)
         fresh = jnp.where((row_lane == 0) | (ids != before), 1.0, 0.0)
-        for p in range(2):
-            starts[2 * j + p] = fresh[:, p * R : (p + 1) * R]
+        for p in range(PER):
+            starts[PER * j + p] = fresh[:, p * R : (p + 1) * R]
             here = ids[:, p * R : (p + 1) * R]
-            onehot[2 * j + p] = jnp.where(
+            onehot[PER * j + p] = jnp.where(
                 jnp.broadcast_to(here, (NCONE, R)) == labels, 1.0, 0.0
             ).astype(BF16)
 
@@ -141,17 +146,25 @@
         pltpu.make_async_copy(rhs_v.at[i], rhs_v.at[i], load_r.at[i]).wait()
     pl.semaphore_wait(barrier, NS - 1 + NC - 1)
 
+    def other(step):
+        z, x, y = step
+        across_x = lax.rem(place // 4 + x, 4)
+        across_y = lax.rem(lax.rem(place, 4) + y, 4)
+        return lax.rem(plane + z, 2) * NP + across_x * 4 + across_y
+
     def to_scens(source, target, sems):
-        for d in range(1, NS):
-            p = lax.rem(me + d, NS)
+        for step in STEPS:
+            p = other(step)
             pltpu.make_async_remote_copy(
                 source(p), target.at[me], scen_sem.at[sems], scen_sem.at[sems + 1],
                 device_id={"scen": p}, device_id_type=MESH,
             ).start()
 
     def to_plane(buffer, sems):
-        for d in range(1, NP):
-            p = plane * NP + lax.rem(place + d, NP)
+        for step in STEPS:
+            if step[0]:
+                continue
+            p = other(step)
             pltpu.make_async_remote_copy(
                 buffer.at[place], buffer.at[place], scen_sem.at[sems], scen_sem.at[sems + 1],
                 device_id={"scen": p}, device_id_type=MESH,
@@ -227,7 +240,7 @@
     def project():
         for j in range(2):
             sums = jnp.zeros((4 * BATCH, NCONE), F32)
-            for i in (2 * j, 2 * j + 1):
+            for i in range(PER * j, PER * j + PER):
                 values = rhs_v[i] - image[i] - dual[i]
                 start = jnp.broadcast_to(starts[i], (BATCH, R))
                 lead_high, lead_low = two_parts(values * start)
@@ -243,7 +256,7 @@
             head = jnp.where(inside, lead, jnp.where(polar, 0.0, middle))
             scale = jnp.where(inside, 1.0, jnp.where(polar, 0.0, middle / safe))
             factors = jnp.concatenate([*two_parts(head), *two_parts(scale)], axis=0)
-            for i in (2 * j, 2 * j + 1):
+            for i in range(PER * j, PER * j + PER):
                 values = rhs_v[i] - image[i] - dual[i]
                 start = jnp.broadcast_to(starts[i], (BATCH, R))
                 spread = dot(factors, onehot[i])
@@ -279,6 +292,12 @@
 
             rows_copy(i).start()
 
+            if i == CH - 1:
+
+                @pl.when(jnp.logical_not(first))
+                def _():
+                    curv_to_partner()
+
             @pl.when(t == 0)
             def _(i=i):
                 pltpu.make_async_copy(T.at[i], T.at[i], load_t.at[i]).wait()
@@ -291,7 +310,7 @@
 
         @pl.when(jnp.logical_not(first))
         def _():
-            curv_to_partner()
+            curv_to_scens()
 
         total = bx[...] + theirs(CH - 1)
         for b in range(2):
@@ -301,10 +320,6 @@
         to_scens(lambda p: rs_send.at[lax.rem(p, NP)], rs_recv, 0)
         rs_recv[me] = rs_send[place]
 
-        @pl.when(jnp.logical_not(first))
-        def _():
-            curv_to_scens()
-
         @pl.when(t == 0)
         def _():
             for i in range(2 * CH):
@@ -321,8 +336,8 @@
 
         for j in range(4):
             rows = vown if j < 2 else vpart
-            a = 2 * (j % 2)
-            by[j] = dot(rows[a], W[2 * j]) + dot(rows[a + 1], W[2 * j + 1])
+            a = PER * (j % 2)
+            by[j] = sum(dot(rows[a + p], W[PER * j + p]) for p in range(PER))
 
         @pl.when(first)
         def _():
@@ -331,14 +346,6 @@
         @pl.when(jnp.logical_not(first))
         def _():
             set_alpha()
-
-        all_came(rs_recv, scen_sem.at[1])
-        back = jnp.sum(rs_recv[...].astype(F32), axis=0)
-        res = rx[...] - alpha[rows16, :] * (dx[...] + back)
-        rx[...] = res
-        ag[place] = res.astype(BF16)
-        to_plane(ag, 4)
-        all_came(rs_recv, scen_sem.at[0])
 
         norm = jnp.zeros((BATCH, 128), F32)
         for j in range(4):
@@ -347,17 +354,24 @@
             ly[j] = r.astype(BF16)
             norm = norm + fold(r * r)
         sq_dir[...] = norm
+
+        all_came(rs_recv, scen_sem.at[1])
+        back = jnp.sum(rs_recv[...].astype(F32), axis=0)
+        res = rx[...] - alpha[rows16, :] * (dx[...] + back)
+        rx[...] = res
+        ag[place] = res.astype(BF16)
+        to_plane(ag, 4)
         sq_dir[rows16, :] += 0.5 * (res * res)
         norm_all[me] = to_row(sq_dir[...])
         to_scens(lambda p: norm_all.at[me], norm_all, 6)
         add_steps()
+        all_came(rs_recv, scen_sem.at[0])
         for i in range(CH):
             rows_copy(i).wait_send()
         for i in range(CH):
-            pps[i] = dot(ly[2 + i // 2], WT[CH + i])
-            own[i] = dot(ly[i // 2], WT[i])
+            pps[i] = dot(ly[2 + i // PER], WT[CH + i])
+            own[i] = dot(ly[i // PER], WT[i])
         all_came(ag, scen_sem.at[5])
-        all_came(ag, scen_sem.at[4])
         for b in range(2):
             for c in range(8):
                 lx[b * 16 : b * 16 + 16, c * 128 : c * 128 + 128] = ag[b * 8 + c]
@@ -375,13 +389,14 @@
             own[i] += dot(lx[...], TT[i])
             if i:
                 exchange(i - 1)
-            if i == 1:
+            if i == PER // 2:
                 all_came(norm_all, scen_sem.at[7])
                 all_came(norm_all, scen_sem.at[6])
                 norm_col[col] = jnp.sum(norm_all[...], axis=0)
                 to_cols(norm_col, 2)
         exchange(CH - 1)
 
+        all_came(ag, scen_sem.at[4])
         all_came(norm_col, col_sem.at[3])
         all_came(norm_col, col_sem.at[2])
         new_norm = jnp.sum(norm_col[...], axis=0)
@@ -435,13 +450,17 @@
 
     lax.fori_loop(0, ITERS * CG_STEPS, iteration, 0)
 
-    quarter = col // 2
-    lanes_here = pl.ds(pl.multiple_of(core * 512, 128), 512)
-    lanes_there = pl.ds(pl.multiple_of((1 - core) * 512, 128), 512)
+    if PER == 2:
+        here = there = col // 2
+        lanes_here = pl.ds(pl.multiple_of(core * 512, 128), 512)
+        lanes_there = pl.ds(pl.multiple_of((1 - core) * 512, 128), 512)
+    else:
+        here, there = col, partner
+        lanes_here = lanes_there = slice(None)
 
     def last_copy(a, j):
         return pltpu.make_async_remote_copy(
-            (slack, dual)[a].at[2 * j + quarter, :, lanes_there], fin.at[a, j],
+            (slack, dual)[a].at[PER * j + there, :, lanes_there], fin.at[a, j],
             fin_sem.at[0, a, j], fin_sem.at[1, a, j],
             device_id={"col": partner}, device_id_type=MESH,
         )
@@ -450,8 +469,8 @@
         for j in range(2):
             last_copy(a, j).start()
     for j in range(2):
-        slack_out[core * 2 + j] = slack[2 * j + quarter, :, lanes_here]
-        dual_out[core * 2 + j] = dual[2 * j + quarter, :, lanes_here]
+        slack_out[core * 2 + j] = slack[PER * j + here, :, lanes_here]
+        dual_out[core * 2 + j] = dual[PER * j + here, :, lanes_here]
         second_out[core * 2 + j] = y[j]
         second_out[(1 - core) * 2 + j] = y[2 + j]
     for a in range(2):

time: 255 us -> 247 us (0.969)
  Pallas kernels: 254 us -> 246 us
    pallas_call x1, Pallas kernels: 252 us -> 244 us  [body(): pl.pallas_call(kernel, out_shape=(jax.ShapeDtypeStruct((BATCH, 1024), F32...]
where the time goes in v3:
time: 247 us; the launch traced here: 246 us
  Pallas kernels  246 us (100%)
    pallas_call x1, Pallas kernels, body(): pl.pallas_call(kernel, out_shape=(jax.ShapeDtypeStruct((BATCH, 1024), F32...  244 us

profile of v3, /device:TPU:0, one launch (start us, length us, event | category | flops | bytes accessed | tf_op | source)
XLA Modules:
  0.0 246.3 jit_solution(2418353392672441416)
XLA Ops:
  0.6 243.6 %shard_map.93 = (f32[32,1024]{1,0:T(8,128)}, f32[4,32,256]{2,1,0:T(8,128)}, f32[4,32,512]{2,1,0:T(8,128)}, f32[4,32,512]{2,1,0:T(8,128)}) custom-call(bf16[4,2048,1024]{2,1,0:T(8,128)(2,1)} %tech.1, bf16[4,2048,256]{2,1,0:T(8,128)(2,1)} %recourse.1, f32[32,4,2048]{2,1,0:T(4,128)} %rhs.1, f32[8,1,128]{2,1,0:T(1,128)} %bitcast.1, f32[4,256]{1,0:T(4,128)} %cost_second.1, ...), custom_call_target="tpu_custom_call" | custom-call | tf_op jit(solution)/shard_map/pallas_call | solution.py:503
  244.2 2.1 shard_map.94

commit v4 on v3

--- a/solution.py
+++ b/solution.py
@@ -64,23 +64,19 @@
     cg = lax.rem(place, 8)
     rows16 = pl.ds(pl.multiple_of((place // 8) * 16, 16), 16)
 
+    def fetch(source, target, sem, i):
+        scen = (core if i < CH else 1 - core) * 2 + i % CH // PER
+        part = pl.ds((i % PER) * R, R)
+        pltpu.make_async_copy(source.at[scen, part], target.at[i], sem.at[i]).start()
+
     for i in range(CH):
-        for half in range(2):
-            scen = (core if half == 0 else 1 - core) * 2 + i // PER
-            part = pl.ds((i % PER) * R, R)
-            pltpu.make_async_copy(
-                tech.at[scen, part], T.at[half * CH + i], load_t.at[half * CH + i]
-            ).start()
         pltpu.make_async_copy(
             rhs.at[:, core * 2 + i // PER, pl.ds((i % PER) * R, R)], rhs_v.at[i], load_r.at[i]
         ).start()
-    for i in range(CH):
-        for half in range(2):
-            scen = (core if half == 0 else 1 - core) * 2 + i // PER
-            part = pl.ds((i % PER) * R, R)
-            pltpu.make_async_copy(
-                recourse.at[scen, part], W.at[half * CH + i], load_w.at[half * CH + i]
-            ).start()
+    for i in (0, 1, 2, 4, 5, 3, 6, 7):
+        fetch(tech, T, load_t, i)
+    for i in range(2 * CH):
+        fetch(recourse, W, load_w, i)
 
     barrier = pltpu.get_barrier_semaphore()
     for d in range(1, NS):
@@ -152,19 +148,19 @@
         across_y = lax.rem(lax.rem(place, 4) + y, 4)
         return lax.rem(plane + z, 2) * NP + across_x * 4 + across_y
 
+    others = [other(step) for step in STEPS]
+
     def to_scens(source, target, sems):
-        for step in STEPS:
-            p = other(step)
+        for p in others:
             pltpu.make_async_remote_copy(
                 source(p), target.at[me], scen_sem.at[sems], scen_sem.at[sems + 1],
                 device_id={"scen": p}, device_id_type=MESH,
             ).start()
 
     def to_plane(buffer, sems):
-        for step in STEPS:
+        for step, p in zip(STEPS, others):
             if step[0]:
                 continue
-            p = other(step)
             pltpu.make_async_remote_copy(
                 buffer.at[place], buffer.at[place], scen_sem.at[sems], scen_sem.at[sems + 1],
                 device_id={"scen": p}, device_id_type=MESH,
@@ -265,54 +261,61 @@
                 slack[i] = new
                 dual[i] = dual[i] + image[i] + new - rhs_v[i]
 
+    def turn_tech(low, high):
+        def turned(i, carry):
+            for b in range(0, R, 256):
+                for c in range(0, 1024, 256):
+                    TT[i, c : c + 256, b : b + 256] = T[i, b : b + 256, c : c + 256].T
+            return carry
+
+        lax.fori_loop(low, high, turned, 0)
+
     def iteration(t, carry):
         k = lax.rem(t, CG_STEPS)
         first = k == 0
         turn = lax.rem(t, 2)
         sq[...] = jnp.zeros((BATCH, 128), F32)
 
-        def theirs(i):
-            rows_copy(i).wait_recv()
+        def here(i):
+            @pl.when(first)
+            def _():
+                vown[i] = (rhs_v[i] - slack[i] - dual[i] - image[i]).astype(BF16)
+
+            @pl.when(jnp.logical_not(first))
+            def _():
+                vown[i] = next_image_step(i, 1 - turn).astype(BF16)
+
+            rows_copy(i).start()
+
+        def adjoint(mine, theirs):
+            for i in theirs:
+                rows_copy(i).wait_recv()
 
             @pl.when(t == 0)
             def _():
-                pltpu.make_async_copy(T.at[CH + i], T.at[CH + i], load_t.at[CH + i]).wait()
-
-            return dot(vpart[i], T[CH + i])
-
-        for i in range(CH):
-
-            @pl.when(first)
-            def _(i=i):
-                vown[i] = (rhs_v[i] - slack[i] - dual[i] - image[i]).astype(BF16)
-
-            @pl.when(jnp.logical_not(first))
-            def _(i=i):
-                vown[i] = next_image_step(i, 1 - turn).astype(BF16)
-
-            rows_copy(i).start()
-
-            if i == CH - 1:
-
-                @pl.when(jnp.logical_not(first))
-                def _():
-                    curv_to_partner()
-
-            @pl.when(t == 0)
-            def _(i=i):
-                pltpu.make_async_copy(T.at[i], T.at[i], load_t.at[i]).wait()
-
-            if i == 0:
-                bx[...] = dot(vown[i], T[i])
-            else:
-                bx[...] += dot(vown[i], T[i])
-                bx[...] += theirs(i - 1)
+                for c in (*mine, *(CH + i for i in theirs)):
+                    pltpu.make_async_copy(T.at[c], T.at[c], load_t.at[c]).wait()
+
+            return sum([dot(vown[i], T[i]) for i in mine] + [dot(vpart[i], T[CH + i]) for i in theirs])
+
+        here(0)
+        here(1)
+        bx[...] = adjoint((0, 1), ())
+        here(2)
+        bx[...] += adjoint((2,), (0, 1))
+        here(3)
 
         @pl.when(jnp.logical_not(first))
         def _():
+            curv_to_partner()
+
+        bx[...] += adjoint((3,), (2,))
+
+        @pl.when(jnp.logical_not(first))
+        def _():
             curv_to_scens()
 
-        total = bx[...] + theirs(CH - 1)
+        total = bx[...] + adjoint((), (CH - 1,))
         for b in range(2):
             for c in range(8):
                 tile = total[b * 16 : b * 16 + 16, c * 128 : c * 128 + 128]
@@ -327,12 +330,11 @@
 
             def turned(i, carry):
                 for b in range(0, R, 256):
-                    for c in range(0, 1024, 256):
-                        TT[i, c : c + 256, b : b + 256] = T[i, b : b + 256, c : c + 256].T
                     WT[i, :, b : b + 256] = W[i, b : b + 256, :].T
                 return carry
 
             lax.fori_loop(0, 2 * CH, turned, 0)
+            turn_tech(0, CH + 1)
 
         for j in range(4):
             rows = vown if j < 2 else vpart
@@ -371,6 +373,11 @@
         for i in range(CH):
             pps[i] = dot(ly[2 + i // PER], WT[CH + i])
             own[i] = dot(ly[i // PER], WT[i])
+
+        @pl.when(t == 0)
+        def _():
+            turn_tech(CH + 1, 2 * CH)
+
         all_came(ag, scen_sem.at[5])
         for b in range(2):
             for c in range(8):
@@ -383,19 +390,30 @@
             zs[i] = here.astype(BF16)
             across_copy(i, turn).start()
 
-        for i in range(CH):
+        def for_partner(i):
             pps[i] += dot(lx[...], TT[CH + i])
             partial_copy(i).start()
+
+        def for_here(i):
             own[i] += dot(lx[...], TT[i])
-            if i:
-                exchange(i - 1)
-            if i == PER // 2:
-                all_came(norm_all, scen_sem.at[7])
-                all_came(norm_all, scen_sem.at[6])
-                norm_col[col] = jnp.sum(norm_all[...], axis=0)
-                to_cols(norm_col, 2)
-        exchange(CH - 1)
-
+
+        for_partner(0)
+        for_here(0)
+        for_partner(1)
+        exchange(0)
+        for_partner(2)
+        for_here(1)
+        exchange(1)
+        all_came(norm_all, scen_sem.at[7])
+        norm_col[col] = jnp.sum(norm_all[...], axis=0)
+        to_cols(norm_col, 2)
+        for_partner(3)
+        for_here(2)
+        exchange(2)
+        for_here(3)
+        exchange(3)
+
+        all_came(norm_all, scen_sem.at[6])
         all_came(ag, scen_sem.at[4])
         all_came(norm_col, col_sem.at[3])
         all_came(norm_col, col_sem.at[2])

time: 247 us -> 243 us (0.984)
  Pallas kernels: 246 us -> 242 us
    pallas_call x1, Pallas kernels: 244 us -> 240 us  [body(): pl.pallas_call(kernel, out_shape=(jax.ShapeDtypeStruct((BATCH, 1024), F32...]
where the time goes in v4:
time: 243 us
  Pallas kernels  242 us (100%)
    pallas_call x1, Pallas kernels, body(): pl.pallas_call(kernel, out_shape=(jax.ShapeDtypeStruct((BATCH, 1024), F32...  240 us

profile of v4, /device:TPU:0, one launch (start us, length us, event | category | flops | bytes accessed | tf_op | source)
XLA Modules:
  0.0 243.0 jit_solution(15058656069187057476)
XLA Ops:
  0.6 240.2 %shard_map.93 = (f32[32,1024]{1,0:T(8,128)}, f32[4,32,256]{2,1,0:T(8,128)}, f32[4,32,512]{2,1,0:T(8,128)}, f32[4,32,512]{2,1,0:T(8,128)}) custom-call(bf16[4,2048,1024]{2,1,0:T(8,128)(2,1)} %tech.1, bf16[4,2048,256]{2,1,0:T(8,128)(2,1)} %recourse.1, f32[32,4,2048]{2,1,0:T(4,128)} %rhs.1, f32[8,1,128]{2,1,0:T(1,128)} %bitcast.1, f32[4,256]{1,0:T(4,128)} %cost_second.1, ...), custom_call_target="tpu_custom_call" | custom-call | tf_op jit(solution)/shard_map/pallas_call | solution.py:521
  240.9 2.1 shard_map.94
